TPU v7x, 32 devices: a whole 2x2x4 slice. The times are simulated.
32 devices in a mesh: psg: 8 (over z, x), head: 4 (over y, core).
Axes of the slice: x: 2, y: 2, z: 4, core: 2. Of those that a mesh axis runs over, the one named last changes fastest.
Arguments:
- queries: bfloat16 [64, 2048], P('psg', 'head'), may hold values from -16 to 16
- passage_keys: bfloat16 [16, 256, 2048], P('psg', None, 'head'), may hold values from -6 to 6
- passage_values: bfloat16 [16, 256, 2048], P('psg', None, 'head'), may hold values from -6 to 6
- shelf_ids: int32 [64, 4], P('psg'), may hold values from 0 to 7, all different within a row; in each aligned block of 8 rows (0 to 7, 8 to 15, ...) at most 8 rows name the same one
- live_mask: int32 [64, 8], P('psg'), may hold values 0 or 1
- w_out: bfloat16 [2048, 2048], P('head'), may hold values from -0.75 to 0.75
Outputs:
- out: bfloat16 [64, 2048], P('psg', 'head')
Inputs may be any that keep to these rules, and one draw needn't show every extreme that they name: `shelf_ids`: each row names 4 different shelves. Among the rows of one device, no shelf is named by more than 8 rows, and in some devices one shelf is named by exactly 8 rows.
All inputs are finite; a program needn't handle non-finite values. No bound on the sum of `live_mask` on one device may be relied on, other than what follows from the above.
Results may differ from a plain program's by a relative error of at most 0.0085.
Values may be sent and summed in bfloat16 or wider, within the bound.
A program may use at most 64 MiB of HBM per device.

v0:
```python
import jax
import jax.numpy as jnp
from jax import lax
from jax.sharding import PartitionSpec as P

DK = 64


far_below = -1e30


def shelf_partials(query_rows, live_bits, passage_keys, passage_values):
    row_count = query_rows.shape[0]
    heads_here = query_rows.shape[1] // DK
    passages_here = passage_keys.shape[0]
    length = passage_keys.shape[1]
    query_heads = query_rows.reshape(row_count, heads_here, DK).transpose(1, 0, 2)
    key_heads = passage_keys.reshape(passages_here * length, heads_here, DK).transpose(1, 0, 2)
    value_heads = passage_values.reshape(passages_here * length, heads_here, DK).transpose(1, 0, 2)
    key_live = jnp.repeat(live_bits > 0, length, axis=1)

    def one_head(operands):
        query_head, key_head, value_head = operands
        scores = jnp.dot(query_head, key_head.T, preferred_element_type=jnp.float32)
        scores = jnp.where(key_live, scores, far_below)
        peak_score = jnp.max(scores, axis=1)
        exp_scores = jnp.exp(scores - peak_score[:, None])
        exp_total = jnp.sum(exp_scores, axis=1)
        weights = exp_scores.astype(jnp.bfloat16)
        context = (
            jnp.dot(weights, value_head, preferred_element_type=jnp.float32) / exp_total[:, None]
        )
        return (context, peak_score, exp_total)

    context, peak_score, exp_total = lax.map(one_head, (query_heads, key_heads, value_heads))
    return (
        context.transpose(1, 0, 2).reshape(row_count, heads_here * DK),
        peak_score.T,
        exp_total.T,
    )


def merge_shelves(context, peak_score, exp_total, has_live):
    request_count, shelf_count, heads_here = peak_score.shape
    masked_peak = jnp.where(has_live[:, :, None], peak_score, far_below)
    best_peak = jnp.max(masked_peak, axis=1)
    shelf_share = jnp.where(
        has_live[:, :, None], exp_total * jnp.exp(masked_peak - best_peak[:, None, :]), 0.0
    )
    context_heads = context.reshape(request_count, shelf_count, heads_here, DK)
    attended = (
        jnp.sum(shelf_share[:, :, :, None] * context_heads, axis=1)
        / jnp.sum(shelf_share, axis=1)[:, :, None]
    )
    return attended.reshape(request_count, heads_here * DK).astype(jnp.bfloat16)


def per_device(queries, passage_keys, passage_values, shelf_ids, live_mask, w_out):
    owners = lax.axis_size("psg")
    requests_here, shelves = shelf_ids.shape
    passages_here = passage_keys.shape[0]
    hidden_width = queries.shape[1]
    capacity = max(2, min(requests_here, 2 * requests_here * shelves // owners))
    first_entry = (jnp.arange(live_mask.shape[1], dtype=jnp.int32) == 0).astype(jnp.int32)
    live_bits = jnp.maximum(live_mask, first_entry[None, :]).reshape(
        requests_here, shelves, passages_here
    )
    owner_ids = jnp.arange(owners, dtype=jnp.int32)
    presence = jnp.sum(
        (shelf_ids[:, :, None] == owner_ids[None, None, :]).astype(jnp.int32), axis=1
    )
    rank_table = jnp.cumsum(presence, axis=0) - presence
    slot_index = jnp.take_along_axis(rank_table, shelf_ids, axis=1)
    box_index = (shelf_ids * capacity + slot_index).reshape(-1)
    repeated = jnp.broadcast_to(
        queries[:, None, :], (requests_here, shelves, hidden_width)
    ).reshape(-1, hidden_width)
    query_box = (
        jnp.zeros((owners * capacity, hidden_width), jnp.bfloat16).at[box_index].set(repeated)
    )
    query_box = query_box.reshape(owners, capacity, hidden_width)
    live_box = (
        jnp.zeros((owners * capacity, passages_here), jnp.int32)
        .at[box_index]
        .set(live_bits.reshape(-1, passages_here))
    )
    live_box = live_box.reshape(owners, capacity, passages_here)
    got_queries, got_live = (
        lax.all_to_all(query_box, "psg", split_axis=0, concat_axis=0, tiled=True),
        lax.all_to_all(live_box, "psg", split_axis=0, concat_axis=0, tiled=True),
    )
    senders = got_queries.shape[0]
    slots_here = got_queries.shape[1]
    context, peak_score, exp_total = shelf_partials(
        got_queries.reshape(senders * slots_here, hidden_width),
        got_live.reshape(senders * slots_here, passages_here),
        passage_keys,
        passage_values,
    )
    heads_here = peak_score.shape[1]
    context, peak_score, exp_total = (
        lax.all_to_all(
            context.reshape(senders, slots_here, hidden_width),
            "psg",
            split_axis=0,
            concat_axis=0,
            tiled=True,
        ),
        lax.all_to_all(
            peak_score.reshape(senders, slots_here, heads_here),
            "psg",
            split_axis=0,
            concat_axis=0,
            tiled=True,
        ),
        lax.all_to_all(
            exp_total.reshape(senders, slots_here, heads_here),
            "psg",
            split_axis=0,
            concat_axis=0,
            tiled=True,
        ),
    )
    heads_here = peak_score.shape[2]
    context = context.reshape(owners * capacity, hidden_width)[box_index].reshape(
        requests_here, shelves, hidden_width
    )
    peak_score = peak_score.reshape(owners * capacity, heads_here)[box_index].reshape(
        requests_here, shelves, heads_here
    )
    exp_total = exp_total.reshape(owners * capacity, heads_here)[box_index].reshape(
        requests_here, shelves, heads_here
    )
    has_live = jnp.max(live_bits, axis=2) > 0
    attended = merge_shelves(context, peak_score, exp_total, has_live)
    projected = jnp.dot(attended, w_out, preferred_element_type=jnp.float32)
    return lax.psum_scatter(projected, "head", scatter_dimension=1, tiled=True).astype(jnp.bfloat16)


def solution(mesh):
    in_specs = (
        P("psg", "head"),
        P("psg", None, "head"),
        P("psg", None, "head"),
        P("psg", None),
        P("psg", None),
        P("head", None),
    )
    out_specs = P("psg", "head")
    return jax.shard_map(
        per_device, mesh=mesh, in_specs=in_specs, out_specs=out_specs, check_vma=False
    )
```

profile of v0, /device:TPU:0, one launch (start us, length us, event | category | flops | bytes accessed | tf_op | source)
XLA Modules:
  0.0 109.1 jit_solution(2862363829850313085)
XLA Ops:
  6.5 0.9 convert_reduce_fusion
  7.4 0.7 bitcast_or_fusion
  8.4 0.7 gather_fusion.3
  9.7 0.7 scatter_custom_fusion.1
  10.4 0.7 copy.84
  11.1 7.3 %all-to-all-start.1 = ((s32[8,8,2]{1,2,0:T(2,128)}), s32[8,8,2]{1,2,0:T(2,128)S(1)}, u32[]{:S(2)}, u32[]{:S(2)}) async-start(s32[8,8,2]{1,2,0:T(2,128)} %copy.84), calls=%async_computation.1 | async-start | bytes 16384 | tf_op jit(solution)/shard_map/all_to_all | solution.py:90
  18.5 0.4 copy.80
  18.9 0.3 reshape.122
  19.3 1.3 %copy.81 = bf16[2,256,512]{1,0,2:T(2,128)(2,1)S(1)} copy(bf16[2,256,512]{2,1,0:T(8,128)(2,1)} %param.10) | data formatting | bytes 1048576 | tf_op args[2]
  20.6 1.1 %reshape.125 = bf16[512,8,64]{0,2,1:T(8,128)(2,1)} reshape(bf16[2,256,512]{1,0,2:T(2,128)(2,1)S(1)} %copy.81) | data formatting | bytes 1048576 | tf_op jit(solution)/shard_map/reshape | solution.py:19
  21.7 1.3 %scatter_custom_fusion = bf16[64,512]{1,0:T(8,128)(2,1)} fusion(s32[32]{0:T(128)S(1)} %fusion.28, bf16[32,512]{1,0:T(8,128)(2,1)S(1)} %reshape.167, bf16[]{:T(256)} %constant.30.clone.1), kind=kCustom, calls=%fused_computation.30 | custom fusion | bytes 65538 | tf_op jit(solution)/shard_map/scatter | solution.py:79
  23.0 1.9 %all-to-all-done.1 = s32[8,8,2]{1,2,0:T(2,128)S(1)} async-done(((s32[8,8,2]{1,2,0:T(2,128)}), s32[8,8,2]{1,2,0:T(2,128)S(1)}, u32[]{:S(2)}, u32[]{:S(2)}) %all-to-all-start.1) | async-done | bytes 544 | tf_op jit(solution)/shard_map/all_to_all | solution.py:90
  24.9 4.1 %all-to-all-start = ((bf16[8,8,512]{2,1,0:T(8,128)(2,1)}), bf16[8,8,512]{2,1,0:T(8,128)(2,1)S(1)}, u32[]{:S(2)}, u32[]{:S(2)}) async-start(bf16[8,8,512]{2,1,0:T(8,128)(2,1)} %bitcast.3), calls=%async_computation | async-start | bytes 131072 | tf_op jit(solution)/shard_map/all_to_all | solution.py:89
  29.2 6.8 %all-to-all-done = bf16[8,8,512]{2,1,0:T(8,128)(2,1)S(1)} async-done(((bf16[8,8,512]{2,1,0:T(8,128)(2,1)}), bf16[8,8,512]{2,1,0:T(8,128)(2,1)S(1)}, u32[]{:S(2)}, u32[]{:S(2)}) %all-to-all-start) | async-done | bytes 65568 | tf_op jit(solution)/shard_map/all_to_all | solution.py:89
  36.1 14.1 %while.15 = (s32[]{:T(128)}, f32[8,64,64]{2,1,0:T(8,128)S(1)}, f32[8,64]{1,0:T(8,128)S(1)}, f32[8,64]{1,0:T(8,128)S(1)}, bf16[8,64,64]{2,1,0:T(8,128)(2,1)S(1)},...) while((s32[]{:T(128)}, f32[8,64,64]{2,1,0:T(8,128)S(1)}, ...), condition=%wide.region_8.9_spmd.clone, body=%wide.region_5.8_spmd.clone.sunk | while | flops 8589186 | bytes 709613 | solution.py:35
  36.3 0.2 fusion.42
  36.5 0.2 fusion.43
  36.7 1.1 fusion.44
  38.0 0.2 fusion.42
  38.3 0.2 fusion.43
  38.5 1.1 fusion.44
  39.8 0.2 fusion.42
  40.2 1.1 fusion.44
  41.5 0.2 fusion.42
  42.0 1.1 fusion.44
  43.3 0.2 fusion.42
  43.7 1.1 fusion.44
  45.1 0.2 fusion.42
  45.5 1.1 fusion.44
  46.8 0.2 fusion.42
  47.3 1.1 fusion.44
  48.6 0.2 fusion.42
  49.0 1.1 fusion.44
  50.2 0.7 copy.96
  50.8 3.3 %all-to-all-start.2 = ((f32[8,8,8]{2,1,0:T(8,128)}), f32[8,8,8]{2,1,0:T(8,128)S(1)}, u32[]{:S(2)}, u32[]{:S(2)}) async-start(f32[8,8,8]{2,1,0:T(8,128)} %bitcast.10), calls=%async_computation.2 | async-start | bytes 65536 | tf_op jit(solution)/shard_map/all_to_all | solution.py:116
  54.2 0.7 copy.97
  54.9 5.9 %all-to-all-done.2 = f32[8,8,8]{2,1,0:T(8,128)S(1)} async-done(((f32[8,8,8]{2,1,0:T(8,128)}), f32[8,8,8]{2,1,0:T(8,128)S(1)}, u32[]{:S(2)}, u32[]{:S(2)}) %all-to-all-start.2) | async-done | bytes 2080 | tf_op jit(solution)/shard_map/all_to_all | solution.py:116
  60.8 3.3 %all-to-all-start.3 = ((f32[8,8,8]{2,1,0:T(8,128)}), f32[8,8,8]{2,1,0:T(8,128)S(1)}, u32[]{:S(2)}, u32[]{:S(2)}) async-start(f32[8,8,8]{2,1,0:T(8,128)} %bitcast.14), calls=%async_computation.3 | async-start | bytes 65536 | tf_op jit(solution)/shard_map/all_to_all | solution.py:109
  64.3 0.8 reshape_reshape.14
  65.1 5.7 %all-to-all-done.3 = f32[8,8,8]{2,1,0:T(8,128)S(1)} async-done(((f32[8,8,8]{2,1,0:T(8,128)}), f32[8,8,8]{2,1,0:T(8,128)S(1)}, u32[]{:S(2)}, u32[]{:S(2)}) %all-to-all-start.3) | async-done | bytes 2080 | tf_op jit(solution)/shard_map/all_to_all | solution.py:109
  70.8 3.4 %all-to-all-start.4 = ((f32[8,8,512]{2,1,0:T(8,128)}), f32[8,8,512]{2,1,0:T(8,128)S(1)}, u32[]{:S(2)}, u32[]{:S(2)}) async-start(f32[8,8,512]{2,1,0:T(8,128)} %reshape_reshape.14), calls=%async_computation.4 | async-start | bytes 262144 | tf_op jit(solution)/shard_map/all_to_all | solution.py:102
  74.3 0.6 gather_fusion
  74.9 0.6 gather_fusion.1
  75.6 5.9 %all-to-all-done.4 = f32[8,8,512]{2,1,0:T(8,128)S(1)} async-done(((f32[8,8,512]{2,1,0:T(8,128)}), f32[8,8,512]{2,1,0:T(8,128)S(1)}, u32[]{:S(2)}, u32[]{:S(2)}) %all-to-all-start.4) | async-done | bytes 131104 | tf_op jit(solution)/shard_map/all_to_all | solution.py:102
  81.4 0.6 gather_fusion.2
  82.4 1.0 fusion.32
  83.4 17.5 %reduce-scatter.2.cloned.1.call-done = f32[8,512]{1,0:T(8,128)} async-done(((f32[8,2048]{1,0:T(8,128)}), f32[8,512]{1,0:T(8,128)}) %reduce-scatter.2.cloned.1.call-update) | async-done | bytes 16400 | tf_op jit(solution)/shard_map/reduce_scatter | solution.py:137
  100.9 1.3 %convert_element_type.26 = bf16[8,512]{1,0:T(8,128)(2,1)} convert(f32[8,512]{1,0:T(8,128)} %reduce-scatter.2.cloned.1.call-done) | non-fusion elementwise | flops 4096 | bytes 24576 | tf_op jit(solution)/shard_map/convert_element_type | solution.py:137
  (84 shorter events, 5.0 us)
Async XLA Ops:
  6.5 75.9 %copy-start = (bf16[512,2048]{1,0:T(8,128)(2,1)S(1)}, bf16[512,2048]{1,0:T(8,128)(2,1)}, u32[]{:S(2)}) copy-start(bf16[512,2048]{1,0:T(8,128)(2,1)} %param.13) | copy-start | bytes 6291460
  8.3 0.9 copy-start.2
  8.3 1.1 copy-start.4
  8.3 10.1 %copy-start.3 = (bf16[8,512]{1,0:T(8,128)(2,1)S(1)}, bf16[8,512]{1,0:T(8,128)(2,1)}, u32[]{:S(2)}) copy-start(bf16[8,512]{1,0:T(8,128)(2,1)} %param.8) | copy-start | bytes 24580
  8.4 10.1 %copy-start.1 = (bf16[2,256,512]{2,1,0:T(8,128)(2,1)S(1)}, bf16[2,256,512]{2,1,0:T(8,128)(2,1)}, u32[]{:S(2)}) copy-start(bf16[2,256,512]{2,1,0:T(8,128)(2,1)} %param.9) | copy-start | bytes 1572868
  11.1 13.8 %all-to-all-start.1 = ((s32[8,8,2]{1,2,0:T(2,128)}), s32[8,8,2]{1,2,0:T(2,128)S(1)}, u32[]{:S(2)}, u32[]{:S(2)}) async-start(s32[8,8,2]{1,2,0:T(2,128)} %copy.84), calls=%async_computation.1 | async-start | bytes 16384 | tf_op jit(solution)/shard_map/all_to_all | solution.py:90
  24.9 11.0 %all-to-all-start = ((bf16[8,8,512]{2,1,0:T(8,128)(2,1)}), bf16[8,8,512]{2,1,0:T(8,128)(2,1)S(1)}, u32[]{:S(2)}, u32[]{:S(2)}) async-start(bf16[8,8,512]{2,1,0:T(8,128)(2,1)} %bitcast.3), calls=%async_computation | async-start | bytes 131072 | tf_op jit(solution)/shard_map/all_to_all | solution.py:89
  50.8 10.0 %all-to-all-start.2 = ((f32[8,8,8]{2,1,0:T(8,128)}), f32[8,8,8]{2,1,0:T(8,128)S(1)}, u32[]{:S(2)}, u32[]{:S(2)}) async-start(f32[8,8,8]{2,1,0:T(8,128)} %bitcast.10), calls=%async_computation.2 | async-start | bytes 65536 | tf_op jit(solution)/shard_map/all_to_all | solution.py:116
  60.8 10.0 %all-to-all-start.3 = ((f32[8,8,8]{2,1,0:T(8,128)}), f32[8,8,8]{2,1,0:T(8,128)S(1)}, u32[]{:S(2)}, u32[]{:S(2)}) async-start(f32[8,8,8]{2,1,0:T(8,128)} %bitcast.14), calls=%async_computation.3 | async-start | bytes 65536 | tf_op jit(solution)/shard_map/all_to_all | solution.py:109
  70.8 10.7 %all-to-all-start.4 = ((f32[8,8,512]{2,1,0:T(8,128)}), f32[8,8,512]{2,1,0:T(8,128)S(1)}, u32[]{:S(2)}, u32[]{:S(2)}) async-start(f32[8,8,512]{2,1,0:T(8,128)} %reshape_reshape.14), calls=%async_computation.4 | async-start | bytes 262144 | tf_op jit(solution)/shard_map/all_to_all | solution.py:102
  74.1 26.8 %reduce-scatter.2.cloned.1.call-start = ((), (), s32[]{:S(2)}) async-start(), calls=%async_computation.6 | async-start | bytes 81920 | tf_op jit(solution)/shard_map/reduce_scatter | solution.py:137
Sparse Core Ops, SparseCore 0:
  83.6 17.2 reduce-scatter.1
where the time goes:
time: 110 us; the launch traced here: 109 us
  waiting for transfers between devices  43.6 us (40%)
  starting transfers between devices  21.5 us (20%)
  local copies, waits for them, and re-layouts  13.7 us (12%)
  between operations  13.6 us (12%)
  matrix products  11.5 us (10%)
  other arithmetic  4.94 us (4%)
    reduce_scatter x1, waiting for transfers between devices, per_device(): lax.psum_scatter(projected, 'head', scatter_dimension=1, tiled=True)  17.5 us
    dot_general x8, matrix products, one_head(): jnp.dot(weights, value_head, preferred_element_type=jnp.float32)  8.51 us
    all_to_all x1, starting transfers between devices, per_device(): lax.all_to_all(live_box, 'psg', split_axis=0, concat_axis=0, tiled=True)  7.28 us
    all_to_all x1, waiting for transfers between devices, per_device(): lax.all_to_all(query_box, 'psg', split_axis=0, concat_axis=0, tiled=True)  6.76 us
    all_to_all x1, waiting for transfers between devices, per_device(): lax.all_to_all(exp_total.reshape(senders, slots_here, heads_here), 'psg',...  5.92 us
    all_to_all x1, waiting for transfers between devices, per_device(): lax.all_to_all(context.reshape(senders, slots_here, hidden_width), 'psg',...  5.86 us
    all_to_all x1, waiting for transfers between devices, per_device(): lax.all_to_all(peak_score.reshape(senders, slots_here, heads_here), 'psg'...  5.69 us
    all_to_all x1, starting transfers between devices, per_device(): lax.all_to_all(query_box, 'psg', split_axis=0, concat_axis=0, tiled=True)  4.1 us
  transfers between devices with their start and end apart: 6, of which 6 were waited for; matrix products, arithmetic and copies ran while one was open for 7% of the time, Pallas kernels for 0%

commit v1 on v0

v1 whole, which is shorter than its diff:
```python
import functools

import jax
import jax.numpy as jnp
from jax import lax
from jax.experimental import pallas as pl
from jax.experimental.pallas import tpu as pltpu
from jax.sharding import PartitionSpec as P

DK = 64
far_below = -1e30
LANES = 128
MESH = pl.DeviceIdType.MESH


def each(low, high, body):
    if high - low <= 8:
        for step in range(low, high):
            body(step)
    else:

        @pl.loop(low, high)
        def _(step):
            body(step)


def kernel(
    dims,
    q_hbm,
    k_hbm,
    v_hbm,
    ids_hbm,
    live_hbm,
    w_hbm,
    out_ref,
    k_v,
    v_v,
    w_v,
    ids_v,
    live_v,
    box,
    part,
    stat,
    got_part,
    got_stat,
    rs_out,
    rs_in,
    local_sem,
    q_send,
    q_recv,
    p_send,
    p_recv,
    s_send,
    s_recv,
    r_send,
    r_recv,
):
    owners, groups, rows, width, shelves, passages, length, flag_lanes, group = dims
    me = lax.axis_index("psg")
    my_head = lax.axis_index("head")
    heads = width // DK
    quad = min(256, width)
    quad_heads = quad // DK
    out_cols = w_v.shape[1] // groups

    barrier = pltpu.get_barrier_semaphore()

    def greet_psg(step):
        pl.semaphore_signal(
            barrier, inc=1, device_id={"psg": lax.rem(me + step, owners)}, device_id_type=MESH
        )

    def greet_head(step):
        pl.semaphore_signal(
            barrier,
            inc=1,
            device_id={"head": lax.rem(my_head + step, groups)},
            device_id_type=MESH,
        )

    each(1, owners, greet_psg)
    each(1, groups, greet_head)

    ids_copy = pltpu.make_async_copy(ids_hbm, ids_v, local_sem.at[0])
    live_copy = pltpu.make_async_copy(live_hbm, live_v, local_sem.at[1])
    q_copy = pltpu.make_async_copy(q_hbm, box.at[me, :, pl.ds(0, width)], local_sem.at[2])
    k_copy = pltpu.make_async_copy(k_hbm, k_v, local_sem.at[3])
    v_copy = pltpu.make_async_copy(v_hbm, v_v, local_sem.at[4])
    w_copy = pltpu.make_async_copy(w_hbm, w_v, local_sem.at[5])
    for copy in (ids_copy, live_copy, q_copy, k_copy, v_copy, w_copy):
        copy.start()
    ids_copy.wait()
    live_copy.wait()
    ids = ids_v[...]
    live = live_v[...]
    lane = lax.broadcasted_iota(jnp.int32, (rows, flag_lanes), 1)
    flags = jnp.zeros((rows, flag_lanes), jnp.int32)
    for shelf in range(shelves):
        for p in range(passages):
            entry = shelf * passages + p
            bit = jnp.int32(1) if entry == 0 else live[:, entry : entry + 1]
            flags = jnp.where(lane == ids[:, shelf : shelf + 1] * passages + p, bit, flags)
    q_copy.wait()
    box[me, :, pl.ds(width, flag_lanes)] = flags.astype(jnp.float32).astype(jnp.bfloat16)

    pl.semaphore_wait(barrier, owners + groups - 2)

    def query_copy(peer, source):
        return pltpu.make_async_remote_copy(
            src_ref=box.at[source],
            dst_ref=box.at[source],
            send_sem=q_send.at[peer],
            recv_sem=q_recv.at[source],
            device_id={"psg": peer},
            device_id_type=MESH,
        )

    def part_copy(peer, source):
        return pltpu.make_async_remote_copy(
            src_ref=part.at[peer],
            dst_ref=got_part.at[source],
            send_sem=p_send.at[peer],
            recv_sem=p_recv.at[source],
            device_id={"psg": peer},
            device_id_type=MESH,
        )

    def stat_copy(peer, source):
        return pltpu.make_async_remote_copy(
            src_ref=stat.at[peer],
            dst_ref=got_stat.at[source],
            send_sem=s_send.at[peer],
            recv_sem=s_recv.at[source],
            device_id={"psg": peer},
            device_id_type=MESH,
        )

    def other(step):
        return lax.rem(me + step, owners)

    each(1, owners, lambda step: query_copy(other(step), me).start())
    k_copy.wait()
    v_copy.wait()
    each(1, owners, lambda step: query_copy(me, other(step)).wait_recv())

    block_rows = group * rows
    quad_head = lax.broadcasted_iota(jnp.int32, (block_rows, quad), 1) // DK
    flag_lane = lax.broadcasted_iota(jnp.int32, (block_rows, flag_lanes), 1)
    stat_lane = lax.broadcasted_iota(jnp.int32, (block_rows, LANES), 1)

    def attend(turn):
        first = turn * group
        boxes = box[pl.ds(first, group)].astype(jnp.float32).reshape(block_rows, width + flag_lanes)
        flag = boxes[:, width:]
        bias = []
        for p in range(passages):
            own = jnp.where(flag_lane == me * passages + p, flag, 0.0)
            column = (jnp.sum(own, axis=1, keepdims=True) - 1.0) * -far_below
            bias.append(jnp.concatenate([column] * quad_heads, axis=0))
        stats = jnp.zeros((block_rows, LANES), jnp.float32)
        for g in range(width // quad):
            q = boxes[:, g * quad : (g + 1) * quad]
            spread = jnp.concatenate(
                [jnp.where(quad_head == i, q, 0.0) for i in range(quad_heads)], axis=0
            ).astype(jnp.bfloat16)
            scores = [
                lax.dot_general(
                    spread,
                    k_v[p, :, g * quad : (g + 1) * quad],
                    (((1,), (1,)), ((), ())),
                    preferred_element_type=jnp.float32,
                )
                + bias[p]
                for p in range(passages)
            ]
            peak = functools.reduce(jnp.maximum, scores).max(axis=1, keepdims=True)
            exps = [jnp.exp(s - peak) for s in scores]
            total = functools.reduce(jnp.add, exps).sum(axis=1, keepdims=True)
            mixed = functools.reduce(
                jnp.add,
                [
                    jnp.dot(
                        exps[p].astype(jnp.bfloat16),
                        v_v[p, :, g * quad : (g + 1) * quad],
                        preferred_element_type=jnp.float32,
                    )
                    for p in range(passages)
                ],
            )
            kept = jnp.zeros((block_rows, quad), jnp.float32)
            for i in range(quad_heads):
                span = slice(i * block_rows, (i + 1) * block_rows)
                kept = jnp.where(quad_head == i, mixed[span], kept)
                h = g * quad_heads + i
                stats = jnp.where(stat_lane == h, peak[span], stats)
                stats = jnp.where(stat_lane == heads + h, total[span], stats)
            part[pl.ds(first, group), :, g * quad : (g + 1) * quad] = kept.reshape(
                group, rows, quad
            ).astype(jnp.bfloat16)
        stat[pl.ds(first, group)] = stats.reshape(group, rows, LANES)

    each(0, owners // group, attend)

    def send_back(step):
        part_copy(other(step), me).start()
        stat_copy(other(step), me).start()

    each(1, owners, send_back)
    got_part[me] = part[me]
    got_stat[me] = stat[me]

    def take_back(step):
        stat_copy(me, other(step)).wait_recv()
        part_copy(me, other(step)).wait_recv()

    each(1, owners, take_back)

    every = got_stat[...]
    peaks = every[:, :, :heads]
    totals = every[:, :, heads : 2 * heads]
    scale = jnp.exp(peaks - jnp.max(peaks, axis=0, keepdims=True))
    inverse = 1.0 / jnp.sum(scale * totals, axis=0, keepdims=True)
    share = scale * inverse

    lane_head = lax.broadcasted_iota(jnp.int32, (rows, width), 1) // DK
    attended = jnp.zeros((rows, width), jnp.float32)
    for o in range(owners):
        spread_share = jnp.zeros((rows, width), jnp.float32)
        for h in range(heads):
            spread_share = jnp.where(lane_head == h, share[o, :, h : h + 1], spread_share)
        attended = attended + spread_share * got_part[o].astype(jnp.float32)
    attended = attended.astype(jnp.bfloat16)

    w_copy.wait()

    def project(column):
        cols = pl.ds(pl.multiple_of(column * out_cols, LANES), out_cols)
        return jnp.dot(attended, w_v[:, cols], preferred_element_type=jnp.float32)

    def share_copy(peer, source):
        return pltpu.make_async_remote_copy(
            src_ref=rs_out.at[peer],
            dst_ref=rs_in.at[source],
            send_sem=r_send.at[peer],
            recv_sem=r_recv.at[source],
            device_id={"head": peer},
            device_id_type=MESH,
        )

    for step in range(1, groups):
        peer = lax.rem(my_head + step, groups)
        rs_out[peer] = project(peer).astype(jnp.bfloat16)
        share_copy(peer, my_head).start()
    result = project(my_head)
    for step in range(1, groups):
        source = lax.rem(my_head + step, groups)
        share_copy(my_head, source).wait_recv()
        result = result + rs_in[source].astype(jnp.float32)
    out_ref[...] = result.astype(jnp.bfloat16)

    def drain(step):
        peer = other(step)
        query_copy(peer, me).wait_send()
        part_copy(peer, me).wait_send()
        stat_copy(peer, me).wait_send()

    each(1, owners, drain)
    for step in range(1, groups):
        share_copy(lax.rem(my_head + step, groups), my_head).wait_send()


def per_device(queries, passage_keys, passage_values, shelf_ids, live_mask, w_out):
    owners = lax.axis_size("psg")
    groups = lax.axis_size("head")
    rows, width = queries.shape
    passages, length, _ = passage_keys.shape
    shelves = shelf_ids.shape[1]
    flag_lanes = -(-owners * passages // LANES) * LANES
    group = min(8, owners)
    out_cols = w_out.shape[1] // groups
    dims = (owners, groups, rows, width, shelves, passages, length, flag_lanes, group)
    dma = pltpu.SemaphoreType.DMA
    return pl.pallas_call(
        functools.partial(kernel, dims),
        out_shape=jax.ShapeDtypeStruct((rows, out_cols), jnp.bfloat16),
        in_specs=[pl.BlockSpec(memory_space=pl.ANY)] * 6,
        out_specs=pl.BlockSpec(memory_space=pltpu.VMEM),
        scratch_shapes=[
            pltpu.VMEM(passage_keys.shape, jnp.bfloat16),
            pltpu.VMEM(passage_values.shape, jnp.bfloat16),
            pltpu.VMEM(w_out.shape, jnp.bfloat16),
            pltpu.VMEM(shelf_ids.shape, jnp.int32),
            pltpu.VMEM(live_mask.shape, jnp.int32),
            pltpu.VMEM((owners, rows, width + flag_lanes), jnp.bfloat16),
            pltpu.VMEM((owners, rows, width), jnp.bfloat16),
            pltpu.VMEM((owners, rows, LANES), jnp.float32),
            pltpu.VMEM((owners, rows, width), jnp.bfloat16),
            pltpu.VMEM((owners, rows, LANES), jnp.float32),
            pltpu.VMEM((groups, rows, out_cols), jnp.bfloat16),
            pltpu.VMEM((groups, rows, out_cols), jnp.bfloat16),
            dma((6,)),
            dma((owners,)),
            dma((owners,)),
            dma((owners,)),
            dma((owners,)),
            dma((owners,)),
            dma((owners,)),
            dma((groups,)),
            dma((groups,)),
        ],
        compiler_params=pltpu.CompilerParams(collective_id=0, has_side_effects=True),
    )(queries, passage_keys, passage_values, shelf_ids, live_mask, w_out)


def solution(mesh):
    in_specs = (
        P("psg", "head"),
        P("psg", None, "head"),
        P("psg", None, "head"),
        P("psg", None),
        P("psg", None),
        P("head", None),
    )
    out_specs = P("psg", "head")
    return jax.shard_map(
        per_device, mesh=mesh, in_specs=in_specs, out_specs=out_specs, check_vma=False
    )
```

time: 110 us -> 23.2 us (0.21)
  waiting for transfers between devices: 43.6 us -> 0 us
  starting transfers between devices: 21.5 us -> 0 us
  Pallas kernels: 0 us -> 20.3 us
  between operations: 13.6 us -> 0.01 us
  matrix products: 11.5 us -> 0 us
  local copies, waits for them, and re-layouts: 13.7 us -> 2.64 us
  other arithmetic: 4.94 us -> 0 us
    all_to_all x5 -> x0, waiting for transfers between devices: 26.1 us -> none  [the longest x1 6.76 us: per_device(): lax.all_to_all(query_box, 'psg', split_axis=0, concat_axis=0, tiled=True)]
    all_to_all x5 -> x0, starting transfers between devices: 21.4 us -> none  [the longest x1 7.28 us: per_device(): lax.all_to_all(live_box, 'psg', split_axis=0, concat_axis=0, tiled=True)]
    pallas_call x0 -> x1, Pallas kernels: none -> 20.3 us  [per_device(): pl.pallas_call(functools.partial(kernel, dims), out_shape=jax.ShapeDtypeS...]
    reduce_scatter x1 -> x0, waiting for transfers between devices: 17.5 us -> none  [per_device(): lax.psum_scatter(projected, 'head', scatter_dimension=1, tiled=True)]
    dot_general x17 -> x0, matrix products: 11.5 us -> none  [the longest x8 8.51 us: one_head(): jnp.dot(weights, value_head, preferred_element_type=jnp.float32)]
    reshape x7 -> x0, local copies, waits for them, and re-layouts: 3.63 us -> none  [the longest x1 1.12 us: shelf_partials(): passage_values.reshape(passages_here * length, heads_here, DK)]
    gather x8 -> x0, local copies, waits for them, and re-layouts: 2.74 us -> none  [the longest x5 1 us: per_device(): slot_index = jnp.take_along_axis(rank_table, shelf_ids, axis=1)]
    reduce_sum x10 -> x0, other arithmetic: 2.59 us -> none  [the longest x8 1.58 us: one_head(): exp_total = jnp.sum(exp_scores, axis=1)]
  transfers between devices with their start and end apart: 6 -> 0, of which waited for: 6 -> 0; matrix products, arithmetic and copies ran while one was open for 7% -> 0% of each run, Pallas kernels for 0% -> 0%
where the time goes in v1:
time: 23.2 us; the launch traced here: 23 us
  Pallas kernels  20.3 us (88%)
  local copies, waits for them, and re-layouts  2.64 us (11%)
    pallas_call x1, Pallas kernels, per_device(): pl.pallas_call(functools.partial(kernel, dims), out_shape=jax.ShapeDtypeS...  20.3 us
    unnamed x2, local copies, waits for them, and re-layouts  2.64 us

profile of v1, /device:TPU:0, one launch (start us, length us, event | category | flops | bytes accessed | tf_op | source)
XLA Modules:
  0.0 23.0 jit_solution(8813476127682843252)
XLA Ops:
  0.0 1.3 %copy.7.ids_hbm = s32[8,4]{1,0:T(8,128)} copy(s32[8,4]{0,1:T(4,128)} %param.9) | data formatting | bytes 256 | tf_op args[3]
  1.3 20.3 %shard_map.64 = bf16[8,512]{1,0:T(8,128)(2,1)} custom-call(bf16[8,512]{1,0:T(8,128)(2,1)} %q_hbm.1, bf16[2,256,512]{2,1,0:T(8,128)(2,1)} %k_hbm.1, bf16[2,256,512]{2,1,0:T(8,128)(2,1)} %v_hbm.1, s32[8,4]{1,0:T(8,128)} %copy.7.ids_hbm, s32[8,8]{1,0:T(8,128)} %live_hbm.1, bf16[512,2048]{1,0:T(8,128)(2,1)} %w_hbm.1), custom_call_target="tpu_custom_call" | custom-call | tf_op jit(solution)/shard_map/pallas_call | solution.py:283
  21.7 1.3 %copy.9 = bf16[8,512]{1,0:T(8,128)(2,1)} copy(bf16[8,512]{1,0:T(8,128)(2,1)} %shard_map.64) | data formatting | bytes 16384

commit v2 on v1

--- a/solution.py
+++ b/solution.py
@@ -8,7 +8,7 @@
 from jax.sharding import PartitionSpec as P
 
 DK = 64
-far_below = -1e30
+far_below = -(2.0**100)
 LANES = 128
 MESH = pl.DeviceIdType.MESH
 
@@ -22,6 +22,15 @@
         @pl.loop(low, high)
         def _(step):
             body(step)
+
+
+def flip(index, mask):
+    bit = 1
+    while bit <= mask:
+        if mask & bit:
+            index = index + bit * (1 - 2 * (index // bit % 2))
+        bit *= 2
+    return index
 
 
 def kernel(
@@ -40,9 +49,7 @@
     live_v,
     box,
     part,
-    stat,
     got_part,
-    got_stat,
     rs_out,
     rs_in,
     local_sem,
@@ -50,8 +57,6 @@
     q_recv,
     p_send,
     p_recv,
-    s_send,
-    s_recv,
     r_send,
     r_recv,
 ):
@@ -91,15 +96,28 @@
         copy.start()
     ids_copy.wait()
     live_copy.wait()
-    ids = ids_v[...]
+    ids_row = ids_v[...].astype(jnp.float32)
+    square = (rows, rows)
+    on_diagonal = lax.broadcasted_iota(jnp.int32, square, 0) == lax.broadcasted_iota(
+        jnp.int32, square, 1
+    )
+    ids = [
+        jnp.sum(
+            jnp.where(on_diagonal, jnp.broadcast_to(ids_row[j : j + 1], square), 0.0),
+            axis=1,
+            keepdims=True,
+        ).astype(jnp.int32)
+        for j in range(shelves)
+    ]
     live = live_v[...]
     lane = lax.broadcasted_iota(jnp.int32, (rows, flag_lanes), 1)
     flags = jnp.zeros((rows, flag_lanes), jnp.int32)
+    assert 3 * heads <= LANES
     for shelf in range(shelves):
         for p in range(passages):
             entry = shelf * passages + p
             bit = jnp.int32(1) if entry == 0 else live[:, entry : entry + 1]
-            flags = jnp.where(lane == ids[:, shelf : shelf + 1] * passages + p, bit, flags)
+            flags = jnp.where(lane == ids[shelf] * passages + p, bit, flags)
     q_copy.wait()
     box[me, :, pl.ds(width, flag_lanes)] = flags.astype(jnp.float32).astype(jnp.bfloat16)
 
@@ -125,23 +143,39 @@
             device_id_type=MESH,
         )
 
-    def stat_copy(peer, source):
-        return pltpu.make_async_remote_copy(
-            src_ref=stat.at[peer],
-            dst_ref=got_stat.at[source],
-            send_sem=s_send.at[peer],
-            recv_sem=s_recv.at[source],
-            device_id={"psg": peer},
-            device_id_type=MESH,
-        )
-
-    def other(step):
-        return lax.rem(me + step, owners)
-
-    each(1, owners, lambda step: query_copy(other(step), me).start())
+    turns = owners // group
+    my_turn = me // group
+    my_place = me % group
+
+    def peer_of(turn, place):
+        return (my_turn + turn) % turns * group + (my_place + place) % group
+
+    def each_peer(turn, body):
+        each(0, group, lambda place: body(peer_of(turn, place)))
+
+    def each_near(body):
+        each(1, group, lambda place: body(peer_of(0, place)))
+
+    def send_query(peer):
+        query_copy(peer, me).start()
+
+    def take_query(source):
+        query_copy(me, source).wait_recv()
+
+    def send_part(peer):
+        part_copy(peer, me).start()
+
+    def take_part(source):
+        part_copy(me, source).wait_recv()
+
+    def drain(peer):
+        query_copy(peer, me).wait_send()
+        part_copy(peer, me).wait_send()
+
+    each(1, turns, lambda turn: each_peer(turn, send_query))
+    each_near(send_query)
     k_copy.wait()
     v_copy.wait()
-    each(1, owners, lambda step: query_copy(me, other(step)).wait_recv())
 
     block_rows = group * rows
     quad_head = lax.broadcasted_iota(jnp.int32, (block_rows, quad), 1) // DK
@@ -149,7 +183,7 @@
     stat_lane = lax.broadcasted_iota(jnp.int32, (block_rows, LANES), 1)
 
     def attend(turn):
-        first = turn * group
+        first = (my_turn + turn) % turns * group
         boxes = box[pl.ds(first, group)].astype(jnp.float32).reshape(block_rows, width + flag_lanes)
         flag = boxes[:, width:]
         bias = []
@@ -174,8 +208,10 @@
                 for p in range(passages)
             ]
             peak = functools.reduce(jnp.maximum, scores).max(axis=1, keepdims=True)
+            peak = peak.astype(jnp.bfloat16).astype(jnp.float32)
             exps = [jnp.exp(s - peak) for s in scores]
             total = functools.reduce(jnp.add, exps).sum(axis=1, keepdims=True)
+            coarse = total.astype(jnp.bfloat16).astype(jnp.float32)
             mixed = functools.reduce(
                 jnp.add,
                 [
@@ -193,31 +229,32 @@
                 kept = jnp.where(quad_head == i, mixed[span], kept)
                 h = g * quad_heads + i
                 stats = jnp.where(stat_lane == h, peak[span], stats)
-                stats = jnp.where(stat_lane == heads + h, total[span], stats)
+                stats = jnp.where(stat_lane == heads + h, coarse[span], stats)
+                stats = jnp.where(stat_lane == 2 * heads + h, (total - coarse)[span], stats)
             part[pl.ds(first, group), :, g * quad : (g + 1) * quad] = kept.reshape(
                 group, rows, quad
             ).astype(jnp.bfloat16)
-        stat[pl.ds(first, group)] = stats.reshape(group, rows, LANES)
-
-    each(0, owners // group, attend)
-
-    def send_back(step):
-        part_copy(other(step), me).start()
-        stat_copy(other(step), me).start()
-
-    each(1, owners, send_back)
+        part[pl.ds(first, group), :, width:] = stats.reshape(group, rows, LANES).astype(
+            jnp.bfloat16
+        )
+
+    each_near(take_query)
+    attend(0)
+    each_near(send_part)
     got_part[me] = part[me]
-    got_stat[me] = stat[me]
-
-    def take_back(step):
-        stat_copy(me, other(step)).wait_recv()
-        part_copy(me, other(step)).wait_recv()
-
-    each(1, owners, take_back)
-
-    every = got_stat[...]
+
+    def far_turn(turn):
+        each_peer(turn, take_query)
+        attend(turn)
+        each_peer(turn, send_part)
+
+    each(1, turns, far_turn)
+    each_near(take_part)
+    each(1, turns, lambda turn: each_peer(turn, take_part))
+
+    every = got_part[:, :, width:].astype(jnp.float32)
     peaks = every[:, :, :heads]
-    totals = every[:, :, heads : 2 * heads]
+    totals = every[:, :, heads : 2 * heads] + every[:, :, 2 * heads : 3 * heads]
     scale = jnp.exp(peaks - jnp.max(peaks, axis=0, keepdims=True))
     inverse = 1.0 / jnp.sum(scale * totals, axis=0, keepdims=True)
     share = scale * inverse
@@ -228,7 +265,7 @@
         spread_share = jnp.zeros((rows, width), jnp.float32)
         for h in range(heads):
             spread_share = jnp.where(lane_head == h, share[o, :, h : h + 1], spread_share)
-        attended = attended + spread_share * got_part[o].astype(jnp.float32)
+        attended = attended + spread_share * got_part[o, :, :width].astype(jnp.float32)
     attended = attended.astype(jnp.bfloat16)
 
     w_copy.wait()
@@ -247,26 +284,23 @@
             device_id_type=MESH,
         )
 
-    for step in range(1, groups):
-        peer = lax.rem(my_head + step, groups)
+    if groups & (groups - 1) == 0:
+        partners = [flip(my_head, mask) for mask in range(groups - 1, 0, -1)]
+    else:
+        partners = [lax.rem(my_head + step, groups) for step in range(1, groups)]
+    for peer in partners:
         rs_out[peer] = project(peer).astype(jnp.bfloat16)
         share_copy(peer, my_head).start()
     result = project(my_head)
-    for step in range(1, groups):
-        source = lax.rem(my_head + step, groups)
-        share_copy(my_head, source).wait_recv()
-        result = result + rs_in[source].astype(jnp.float32)
+    for peer in reversed(partners):
+        share_copy(my_head, peer).wait_recv()
+        result = result + rs_in[peer].astype(jnp.float32)
     out_ref[...] = result.astype(jnp.bfloat16)
 
-    def drain(step):
-        peer = other(step)
-        query_copy(peer, me).wait_send()
-        part_copy(peer, me).wait_send()
-        stat_copy(peer, me).wait_send()
-
-    each(1, owners, drain)
-    for step in range(1, groups):
-        share_copy(lax.rem(my_head + step, groups), my_head).wait_send()
+    each_near(drain)
+    each(1, turns, lambda turn: each_peer(turn, drain))
+    for peer in partners:
+        share_copy(peer, my_head).wait_send()
 
 
 def per_device(queries, passage_keys, passage_values, shelf_ids, live_mask, w_out):
@@ -276,31 +310,27 @@
     passages, length, _ = passage_keys.shape
     shelves = shelf_ids.shape[1]
     flag_lanes = -(-owners * passages // LANES) * LANES
-    group = min(8, owners)
+    group = next(size for size in (8, 4, 2, 1) if owners % size == 0 and size < owners)
     out_cols = w_out.shape[1] // groups
     dims = (owners, groups, rows, width, shelves, passages, length, flag_lanes, group)
     dma = pltpu.SemaphoreType.DMA
     return pl.pallas_call(
         functools.partial(kernel, dims),
-        out_shape=jax.ShapeDtypeStruct((rows, out_cols), jnp.bfloat16),
+        out_shape=pltpu.VMEM((rows, out_cols), jnp.bfloat16),
         in_specs=[pl.BlockSpec(memory_space=pl.ANY)] * 6,
         out_specs=pl.BlockSpec(memory_space=pltpu.VMEM),
         scratch_shapes=[
             pltpu.VMEM(passage_keys.shape, jnp.bfloat16),
             pltpu.VMEM(passage_values.shape, jnp.bfloat16),
             pltpu.VMEM(w_out.shape, jnp.bfloat16),
-            pltpu.VMEM(shelf_ids.shape, jnp.int32),
+            pltpu.VMEM((shelves, rows), jnp.int32),
             pltpu.VMEM(live_mask.shape, jnp.int32),
             pltpu.VMEM((owners, rows, width + flag_lanes), jnp.bfloat16),
-            pltpu.VMEM((owners, rows, width), jnp.bfloat16),
-            pltpu.VMEM((owners, rows, LANES), jnp.float32),
-            pltpu.VMEM((owners, rows, width), jnp.bfloat16),
-            pltpu.VMEM((owners, rows, LANES), jnp.float32),
+            pltpu.VMEM((owners, rows, width + LANES), jnp.bfloat16),
+            pltpu.VMEM((owners, rows, width + LANES), jnp.bfloat16),
             pltpu.VMEM((groups, rows, out_cols), jnp.bfloat16),
             pltpu.VMEM((groups, rows, out_cols), jnp.bfloat16),
             dma((6,)),
-            dma((owners,)),
-            dma((owners,)),
             dma((owners,)),
             dma((owners,)),
             dma((owners,)),
@@ -309,7 +339,7 @@
             dma((groups,)),
         ],
         compiler_params=pltpu.CompilerParams(collective_id=0, has_side_effects=True),
-    )(queries, passage_keys, passage_values, shelf_ids, live_mask, w_out)
+    )(queries, passage_keys, passage_values, shelf_ids.T, live_mask, w_out)
 
 
 def solution(mesh):

time: 23.2 us -> 20.4 us (0.88)
  local copies, waits for them, and re-layouts: 2.64 us -> 0.6 us
  Pallas kernels: 20.3 us -> 19.6 us
    unnamed x2 -> x1, local copies, waits for them, and re-layouts: 2.64 us -> 0.6 us
    pallas_call x1, Pallas kernels: 20.3 us -> 19.6 us  [per_device(): pl.pallas_call(functools.partial(kernel, dims), out_shape=pltpu.VMEM((row...]
where the time goes in v2:
time: 20.4 us; the launch traced here: 20.2 us
  Pallas kernels  19.6 us (96%)
  local copies, waits for them, and re-layouts  0.6 us (3%)
    pallas_call x1, Pallas kernels, per_device(): pl.pallas_call(functools.partial(kernel, dims), out_shape=pltpu.VMEM((row...  19.6 us
    unnamed x1, local copies, waits for them, and re-layouts  0.6 us

profile of v2, /device:TPU:0, one launch (start us, length us, event | category | flops | bytes accessed | tf_op | source)
XLA Modules:
  0.0 20.2 jit_solution(10369116270808448028)
XLA Ops:
  0.0 19.6 %shard_map.64 = bf16[8,512]{1,0:T(8,128)(2,1)S(1)} custom-call(bf16[8,512]{1,0:T(8,128)(2,1)} %q_hbm.1, bf16[2,256,512]{2,1,0:T(8,128)(2,1)} %k_hbm.1, bf16[2,256,512]{2,1,0:T(8,128)(2,1)} %v_hbm.1, s32[4,8]{1,0:T(4,128)} %bitcast.1, s32[8,8]{1,0:T(8,128)} %live_hbm.1, bf16[512,2048]{1,0:T(8,128)(2,1)} %w_hbm.1), custom_call_target="tpu_custom_call" | custom-call | tf_op jit(solution)/shard_map/pallas_call | solution.py:317
  19.6 0.6 %copy.8 = bf16[8,512]{1,0:T(8,128)(2,1)} copy(bf16[8,512]{1,0:T(8,128)(2,1)S(1)} %shard_map.64) | data formatting | bytes 16384

commit v3 on v2

--- a/solution.py
+++ b/solution.py
@@ -147,8 +147,13 @@
     my_turn = me // group
     my_place = me % group
 
+    def block_of(turn):
+        if isinstance(turn, int) and turns & (turns - 1) == 0:
+            return flip(my_turn, turn)
+        return (my_turn + turn) % turns
+
     def peer_of(turn, place):
-        return (my_turn + turn) % turns * group + (my_place + place) % group
+        return block_of(turn) * group + (my_place + place) % group
 
     def each_peer(turn, body):
         each(0, group, lambda place: body(peer_of(turn, place)))
@@ -172,7 +177,7 @@
         query_copy(peer, me).wait_send()
         part_copy(peer, me).wait_send()
 
-    each(1, turns, lambda turn: each_peer(turn, send_query))
+    each(1, turns, lambda turn: each_peer(turns - turn, send_query))
     each_near(send_query)
     k_copy.wait()
     v_copy.wait()
@@ -183,7 +188,7 @@
     stat_lane = lax.broadcasted_iota(jnp.int32, (block_rows, LANES), 1)
 
     def attend(turn):
-        first = (my_turn + turn) % turns * group
+        first = block_of(turn) * group
         boxes = box[pl.ds(first, group)].astype(jnp.float32).reshape(block_rows, width + flag_lanes)
         flag = boxes[:, width:]
         bias = []
@@ -259,13 +264,19 @@
     inverse = 1.0 / jnp.sum(scale * totals, axis=0, keepdims=True)
     share = scale * inverse
 
-    lane_head = lax.broadcasted_iota(jnp.int32, (rows, width), 1) // DK
-    attended = jnp.zeros((rows, width), jnp.float32)
+    high_half = lax.broadcasted_iota(jnp.int32, (rows, LANES), 1) // DK
+    per_tile = LANES // DK
+    columns = [jnp.zeros((rows, LANES), jnp.float32) for _ in range(width // LANES)]
     for o in range(owners):
-        spread_share = jnp.zeros((rows, width), jnp.float32)
-        for h in range(heads):
-            spread_share = jnp.where(lane_head == h, share[o, :, h : h + 1], spread_share)
-        attended = attended + spread_share * got_part[o, :, :width].astype(jnp.float32)
+        for c in range(width // LANES):
+            weight = share[o, :, c * per_tile : c * per_tile + 1]
+            for i in range(1, per_tile):
+                h = c * per_tile + i
+                weight = jnp.where(high_half == i, share[o, :, h : h + 1], weight)
+            columns[c] = columns[c] + weight * got_part[
+                o, :, c * LANES : (c + 1) * LANES
+            ].astype(jnp.float32)
+    attended = jnp.concatenate(columns, axis=1)
     attended = attended.astype(jnp.bfloat16)
 
     w_copy.wait()
@@ -310,7 +321,7 @@
     passages, length, _ = passage_keys.shape
     shelves = shelf_ids.shape[1]
     flag_lanes = -(-owners * passages // LANES) * LANES
-    group = next(size for size in (8, 4, 2, 1) if owners % size == 0 and size < owners)
+    group = next(size for size in (8, 4, 2, 1) if owners % (2 * size) == 0 or size == 1)
     out_cols = w_out.shape[1] // groups
     dims = (owners, groups, rows, width, shelves, passages, length, flag_lanes, group)
     dma = pltpu.SemaphoreType.DMA

time: 20.4 us -> 20.4 us (level)
  no operation moved by 1% of the time
where the time goes in v3:
time: 20.4 us; the launch traced here: 20.2 us
  Pallas kernels  19.6 us (96%)
  local copies, waits for them, and re-layouts  0.6 us (3%)
    pallas_call x1, Pallas kernels, per_device(): pl.pallas_call(functools.partial(kernel, dims), out_shape=pltpu.VMEM((row...  19.6 us
    unnamed x1, local copies, waits for them, and re-layouts  0.6 us

profile of v3, /device:TPU:0, one launch (start us, length us, event | category | flops | bytes accessed | tf_op | source)
XLA Modules:
  0.0 20.2 jit_solution(9801187838096087262)
XLA Ops:
  0.0 19.6 %shard_map.64 = bf16[8,512]{1,0:T(8,128)(2,1)S(1)} custom-call(bf16[8,512]{1,0:T(8,128)(2,1)} %q_hbm.1, bf16[2,256,512]{2,1,0:T(8,128)(2,1)} %k_hbm.1, bf16[2,256,512]{2,1,0:T(8,128)(2,1)} %v_hbm.1, s32[4,8]{1,0:T(4,128)} %bitcast.1, s32[8,8]{1,0:T(8,128)} %live_hbm.1, bf16[512,2048]{1,0:T(8,128)(2,1)} %w_hbm.1), custom_call_target="tpu_custom_call" | custom-call | tf_op jit(solution)/shard_map/pallas_call | solution.py:328
  19.6 0.6 %copy.8 = bf16[8,512]{1,0:T(8,128)(2,1)} copy(bf16[8,512]{1,0:T(8,128)(2,1)S(1)} %shard_map.64) | data formatting | bytes 16384
